TPU v7x, 8 devices: a whole 2x2x1 slice. The times are simulated.
8 devices in a mesh: by: 2 (over z, y), bx: 4 (over x, core).
Axes of the slice: x: 2, y: 2, z: 1, core: 2. Of those that a mesh axis runs over, the one named last changes fastest.
Arguments:
- wave_fn: float32 [2048, 2, 2, 2048], P('bx', None, None, 'by')
- left_env: float32 [2048, 5, 2048], P('bx')
- mpo_ten: float32 [5, 2, 2, 5], replicated
- right_env: float32 [2048, 5, 2048], P('by')
Outputs:
- output: float32 [2048, 2, 2, 2048], P('bx', None, None, 'by')
All inputs are finite; a program needn't handle non-finite values.
Results may differ from a plain program's by a relative error of at most 0.001.
Values sent between devices are 32-bit elements.
A program may use at most 1 GiB of HBM per device.

v0:
```python
import jax
import jax.numpy as jnp
from jax import lax
from jax.sharding import PartitionSpec as P


def solution(mesh):
    prec_mode = lax.Precision.HIGHEST

    def local_apply(wave_blk, left_rows, mpo_ten, right_rows):
        row_share, mpo_dim, bond_dim = left_rows.shape
        phys_dim = wave_blk.shape[1]
        col_share = wave_blk.shape[3]
        wave_cols = lax.all_gather(wave_blk, 'bx', axis=0, tiled=True)
        stage_one = jnp.dot(left_rows.reshape(row_share * mpo_dim, bond_dim), wave_cols.reshape(bond_dim, phys_dim * phys_dim * col_share), precision=prec_mode, preferred_element_type=jnp.float32)
        stage_one = stage_one.reshape(row_share, mpo_dim, phys_dim, phys_dim, col_share)
        stage_two = jnp.einsum('aupqf,uspv->asvqf', stage_one, mpo_ten, precision=prec_mode, preferred_element_type=jnp.float32)
        stage_three = jnp.einsum('asvqf,vtqr->astrf', stage_two, mpo_ten, precision=prec_mode, preferred_element_type=jnp.float32)
        right_cols = lax.all_to_all(right_rows, 'by', 2, 0, tiled=True)
        part_sum = lax.dot_general(stage_three.reshape(row_share * phys_dim * phys_dim, mpo_dim * col_share), right_cols.reshape(bond_dim, mpo_dim * col_share), (((1,), (1,)), ((), ())), precision=prec_mode, preferred_element_type=jnp.float32)
        part_sum = part_sum.reshape(row_share, phys_dim, phys_dim, bond_dim)
        return lax.psum_scatter(part_sum, 'by', scatter_dimension=3, tiled=True)

    return jax.shard_map(local_apply, mesh=mesh, in_specs=(P('bx', None, None, 'by'), P('bx', None, None), P(), P('by', None, None)), out_specs=P('bx', None, None, 'by'), check_vma=False)
```

profile of v0, /device:TPU:0, one launch (start us, length us, event | category | flops | bytes accessed | tf_op | source)
XLA Modules:
  0.0 2268.0 jit_solution(7219046608098257827)
XLA Ops:
  6.5 0.0 copy-start
  6.5 0.0 all-gather.2.cloned.1.call-start
  6.5 0.7 all-gather.2.cloned.1.call-update
  7.3 0.0 reduce-scatter.2.cloned.1.call-start
  7.3 55.5 %copy.20 = f32[1024,5,2048]{0,1,2:T(8,128)} copy(f32[1024,5,2048]{2,0,1:T(8,128)} %param.7) | data formatting | bytes 83886080 | tf_op args[3]
  62.8 783.9 %all_to_all.15 = f32[1024,5,2048]{0,1,2:T(8,128)} all-to-all(f32[1024,5,2048]{0,1,2:T(8,128)} %copy.20), channel_id=1, replica_groups=mesh['by'=2,'bx'=4] {'by'}, dimensions={2} | all-to-all | bytes 83886080 | tf_op jit(solution)/shard_map/all_to_all | solution.py:19
  846.6 58.5 %copy.21 = f32[1024,5,2,1024]{0,2,3,1:T(2,128)} copy(f32[1024,5,2,1024]{0,1,3,2:T(8,128)} %bitcast.18) | data formatting | bytes 83886080 | tf_op jit(solution)/shard_map/all_to_all | solution.py:19
  905.1 36.9 %copy.42 = f32[640,8,2,1024]{3,1,2,0:T(8,128)} copy(f32[640,8,2,1024]{3,2,1,0:T(2,128)} %bitcast.53) | data formatting | bytes 83886080
  942.0 0.0 all-gather.2.cloned.1.call-done
  942.0 48.7 %copy.34 = f32[2048,2,2,1024]{0,3,2,1:T(8,128)} copy(f32[2048,2,2,1024]{3,2,1,0:T(2,128)} %all-gather.2.cloned.1.call-done) | data formatting | bytes 67108864 | tf_op jit(solution)/shard_map/reshape | solution.py:15
  990.7 279.8 %fusion.12 = f32[512,5,2,2,1024,1]{4,0,3,2,1,5:T(8,128)} fusion(f32[2048,2,2,1024]{0,3,2,1:T(8,128)} %copy.34, f32[512,5,2048]{2,0,1:T(8,128)} %param.5), kind=kOutput, calls=%fused_computation.10 | convolution fusion | flops 257698037760 | bytes 96468992 | tf_op jit(solution)/shard_map/dot_general | solution.py:15
  1270.4 0.0 copy-done
  1270.4 113.8 %fusion.2 = f32[512,2,1024,2,5,1]{2,4,5,1,3,0:T(8,128)} fusion(f32[512,5,2,2,1024,1]{4,0,3,2,1,5:T(8,128)} %fusion.12, f32[5,2,2,5,1,1]{3,2,1,0,5,4:T(2,128)S(1)} %bitcast.51), kind=kOutput, calls=%fused_computation.2 | convolution fusion | flops 1258291200 | bytes 83886480 | tf_op jit(solution)/shard_map/aupqf,uspv->asvqf/dot_general | solution.py:17
  1384.2 74.0 %fusion.8 = f32[512,2,2,5,1024]{4,3,2,1,0:T(8,128)} fusion(f32[512,2,1024,2,5,1]{2,4,5,1,3,0:T(8,128)} %fusion.2, f32[5,2,2,5,1,1]{3,2,1,0,5,4:T(2,128)S(1)} %bitcast.52), kind=kOutput, calls=%fused_computation.8 | convolution fusion | flops 1258291200 | bytes 83886480 | tf_op jit(solution)/shard_map/asvqf,vtqr->astrf/dot_general | solution.py:18
  1458.2 57.5 %copy.19 = f32[512,2,2,5,1024]{0,4,3,2,1:T(8,128)} copy(f32[512,2,2,5,1024]{4,3,2,1,0:T(8,128)} %fusion.8) | data formatting | bytes 83886080 | tf_op jit(solution)/shard_map/asvqf,vtqr->astrf/transpose | solution.py:18
  1515.7 543.2 %fusion.4 = f32[512,2,2,2048]{3,0,2,1:T(8,128)} fusion(f32[512,2,2,5120]{0,3,2,1:T(8,128)} %bitcast.55, f32[2048,5120]{0,1:T(8,128)} %bitcast.54), kind=kOutput, calls=%fused_computation.4 | convolution fusion | flops 257698037760 | bytes 100663296 | tf_op jit(solution)/shard_map/dot_general | solution.py:20
  2058.9 0.0 reduce-scatter.2.cloned.1.call-update
  2058.9 186.6 %reduce-scatter.2.cloned.1.call-done = f32[512,2,2,1024]{3,0,2,1:T(8,128)} async-done(((f32[512,2,2,2048]{3,0,2,1:T(8,128)}), f32[512,2,2,1024]{3,0,2,1:T(8,128)}) %reduce-scatter.2.cloned.1.call-update) | async-done | bytes 8388624 | tf_op jit(solution)/shard_map/reduce_scatter | solution.py:22
  2245.5 15.4 copy.24
Async XLA Ops:
  6.5 1263.9 %copy-start = (f32[5,2,2,5]{3,2,1,0:T(2,128)S(1)}, f32[5,2,2,5]{3,2,1,0:T(2,128)}, u32[]{:S(2)}) copy-start(f32[5,2,2,5]{3,2,1,0:T(2,128)} %param.6) | copy-start | bytes 1204
  6.5 935.4 %all-gather.2.cloned.1.call-start = ((), (), s32[]{:S(2)}) async-start(), calls=%async_computation.2 | async-start | bytes 41943040 | tf_op jit(solution)/shard_map/all_gather | solution.py:14
  7.3 2238.3 %reduce-scatter.2.cloned.1.call-start = ((), (), s32[]{:S(2)}) async-start(), calls=%async_computation.3 | async-start | bytes 25165824 | tf_op jit(solution)/shard_map/reduce_scatter | solution.py:22
Sparse Core Ops, SparseCore 0:
  8.9 202.1 all-gather.1
  2059.0 186.4 reduce-scatter.1
where the time goes:
time: 2280 us; the launch traced here: 2270 us
  matrix products  1010 us (44%)
  blocking collectives  784 us (34%)
  local copies, waits for them, and re-layouts  272 us (12%)
  waiting for transfers between devices  187 us (8%)
    all_to_all x1, blocking collectives, local_apply(): right_cols = lax.all_to_all(right_rows, 'by', 2, 0, tiled=True)  784 us
    dot_general x1, matrix products, local_apply(): lax.dot_general(stage_three.reshape(row_share * phys_dim * phys_dim, mpo_...  543 us
    dot_general x1, matrix products, local_apply(): jnp.dot(left_rows.reshape(row_share * mpo_dim, bond_dim), wave_cols.resha...  280 us
    reduce_scatter x1, waiting for transfers between devices, local_apply(): return lax.psum_scatter(part_sum, 'by', scatter_dimension=3, tiled=True)  187 us
    dot_general x1, matrix products, local_apply(): jnp.einsum('aupqf,uspv->asvqf', stage_one, mpo_ten, precision=prec_mode,...  114 us
    unnamed x4, local copies, waits for them, and re-layouts  92.4 us
    dot_general x1, matrix products, local_apply(): jnp.einsum('asvqf,vtqr->astrf', stage_two, mpo_ten, precision=prec_mode,...  74 us
    all_to_all x1, local copies, waits for them, and re-layouts, local_apply(): right_cols = lax.all_to_all(right_rows, 'by', 2, 0, tiled=True)  58.5 us
  transfers between devices with their start and end apart: 2, of which 1 were waited for; matrix products, arithmetic and copies ran while one was open for 7% of the time, Pallas kernels for 0%

commit v1 on v0

v1 whole, which is shorter than its diff:
```python
import jax
import jax.numpy as jnp
from jax import lax
from jax.experimental import pallas as pl
from jax.experimental.pallas import tpu as pltpu
from jax.sharding import PartitionSpec as P

HI = lax.Precision.HIGHEST
F32 = jnp.float32
VMEM_LIMIT = 63 * 2**20
MESH = pl.DeviceIdType.MESH
ANY = pl.BlockSpec(memory_space=pl.ANY)


def greet(others):
    barrier = pltpu.get_barrier_semaphore()
    for other in others:
        pl.semaphore_signal(barrier, inc=1, device_id=other, device_id_type=MESH)
    pl.semaphore_wait(barrier, len(others))


def left_kernel(mix_hbm, left, xs, right, t3, t1, xg, rfar, buf, mix, mix_sem, send, recv):
    ta, tf, kb = 128, 256, 512
    by = lax.axis_index("by")
    bx = lax.axis_index("bx")
    core = lax.rem(bx, 2)
    chip = bx - core
    pair_bx = chip + 1 - core
    far_bx = lax.rem(bx + 2, 4)
    farpair_bx = lax.rem(pair_bx + 2, 4)
    pair = (by, pair_bx)
    far = (by, far_bx)
    across = (1 - by, bx)
    greet((pair, far, across))

    def remote(k, src, dst, to):
        return pltpu.make_async_remote_copy(
            src_ref=src, dst_ref=dst, send_sem=send.at[k], recv_sem=recv.at[k], device_id=to, device_id_type=MESH
        )

    to_pair = [remote(h, xs.at[h], xg.at[0, h], pair) for h in range(2)]
    to_far = [remote(2 + h, xs.at[h], xg.at[1, h], far) for h in range(2)]
    on_pair = [remote(4 + h, xg.at[1, h], xg.at[2, h], pair) for h in range(2)]
    rows = pl.ds(pl.multiple_of(core * 512, 512), 512)
    f_far = pl.ds(pl.multiple_of((1 - by) * 1024, 1024), 1024)
    r_across = remote(6, right.at[:, rows, f_far], rfar.at[:, rows, :], across)
    r_pair = remote(7, rfar.at[:, rows, :], rfar.at[:, rows, :], pair)

    to_pair[0].start()
    to_far[0].start()
    r_across.start()
    to_pair[1].start()
    to_far[1].start()
    get_mix = pltpu.make_async_copy(mix_hbm, mix, mix_sem)
    get_mix.start()
    get_mix.wait()

    def product(l0, l1, x0, x1):
        lhs = jnp.concatenate([l0[...].reshape(5 * ta, kb), l1[...].reshape(5 * ta, kb)], axis=1)
        rhs = jnp.concatenate([jnp.concatenate([x[i] for i in range(4)], axis=1) for x in (x0, x1)], axis=0)
        return jnp.dot(lhs, rhs, precision=HI, preferred_element_type=F32)

    def left_spec(col):
        return pl.BlockSpec((5, ta, kb), lambda j, i: (0, i, col))

    x_spec = pl.BlockSpec((4, kb, tf), lambda j, i: (0, 0, j))

    def t_spec(h):
        return pl.BlockSpec((5, 4, ta, tf), lambda j, i: (0, 0, i, 2 * h + j))

    def at_step(n, act):
        if act is not None:
            pl.when(pl.program_id(0) * 4 + pl.program_id(1) == n)(act)

    def first_half(h, n=0, act=None):
        def body(l0, l1, x0, x1, o):
            at_step(n, act)
            d = product(l0, l1, x0, x1)
            for u in range(5):
                for i in range(4):
                    o[u, i] = d[u * ta : (u + 1) * ta, i * tf : (i + 1) * tf]

        pltpu.emit_pipeline(
            body, grid=(2, 4), in_specs=[left_spec(bx), left_spec(pair_bx), x_spec, x_spec], out_specs=[t_spec(h)]
        )(left, left, xs.at[h], xg.at[0, h], t1)

    def second_half(h, n=0, act=None):
        def body(l0, l1, x0, x1, t, o):
            at_step(n, act)
            d = product(l0, l1, x0, x1)
            for u in range(5):
                for i in range(4):
                    buf[u, i] = d[u * ta : (u + 1) * ta, i * tf : (i + 1) * tf] + t[u, i]
            for a0 in range(0, ta, 16):
                m = jnp.concatenate(
                    [
                        jnp.concatenate([buf[u, i, a0 : a0 + 8], buf[u, i, a0 + 8 : a0 + 16]], axis=1)
                        for u in range(5)
                        for i in range(4)
                    ],
                    axis=0,
                )
                z = jnp.dot(mix[...], m, precision=HI, preferred_element_type=F32)
                for r in range(5):
                    for i in range(4):
                        row = (r * 4 + i) * 8
                        o[r, i, a0 : a0 + 8] = z[row : row + 8, :tf]
                        o[r, i, a0 + 8 : a0 + 16] = z[row : row + 8, tf:]

        pltpu.emit_pipeline(
            body,
            grid=(2, 4),
            in_specs=[left_spec(far_bx), left_spec(farpair_bx), x_spec, x_spec, t_spec(h)],
            out_specs=[t_spec(h)],
        )(left, left, xg.at[1, h], xg.at[2, h], t1, t3)

    def hand_on(k):
        def act():
            to_far[k].wait_recv()
            on_pair[k].start()

        return act

    def hand_on_right():
        r_across.wait_recv()
        r_pair.start()

    to_pair[0].wait_recv()
    first_half(0)
    to_pair[1].wait_recv()
    first_half(1, 5, hand_on(0))
    on_pair[0].wait_recv()
    second_half(0, 5, hand_on(1))
    on_pair[1].wait_recv()
    second_half(1, 3, hand_on_right)
    r_pair.wait_recv()
    for c in (*to_pair, *to_far, *on_pair, r_across, r_pair):
        c.wait_send()


def right_kernel(t3, rfar, right, y, held, got, send, recv):
    ta, tb = 128, 512
    by = lax.axis_index("by")
    bx = lax.axis_index("bx")
    across = (1 - by, bx)
    greet((across,))
    slots = held.shape[0]

    def remote(slot, tile):
        return pltpu.make_async_remote_copy(
            src_ref=held.at[slot],
            dst_ref=got.at[tile],
            send_sem=send.at[slot],
            recv_sem=recv.at[tile],
            device_id=across,
            device_id_type=MESH,
        )

    def product(t, b):
        lhs = jnp.concatenate([t[r].reshape(4 * ta, 1024) for r in range(5)], axis=1)
        rhs = jnp.concatenate([b[r] for r in range(5)], axis=1)
        d = lax.dot_general(lhs, rhs, (((1,), (1,)), ((), ())), precision=HI, preferred_element_type=F32)
        return d.reshape(4, ta, tb)

    t_spec = pl.BlockSpec((5, 4, ta, 1024), lambda j, i: (0, 0, i, 0))

    def far_body(t, b):
        tile = pl.program_id(0) * 4 + pl.program_id(1)
        slot = lax.rem(tile, slots)

        @pl.when(tile >= slots)
        def _():
            remote(slot, tile).wait_send()

        held[slot] = product(t, b)
        remote(slot, tile).start()

    pltpu.emit_pipeline(
        far_body,
        grid=(2, 4),
        in_specs=[t_spec, pl.BlockSpec((5, tb, 1024), lambda j, i: (0, j, 0))],
        out_specs=[],
    )(t3, rfar)

    def own_body(t, b, o):
        tile = pl.program_id(0) * 4 + pl.program_id(1)
        d = product(t, b)
        remote(0, tile).wait_recv()
        o[...] = d + got[tile]

    pltpu.emit_pipeline(
        own_body,
        grid=(2, 4),
        in_specs=[t_spec, pl.BlockSpec((5, tb, 1024), lambda j, i: (0, j, by))],
        out_specs=[pl.BlockSpec((4, ta, tb), lambda j, i: (0, i, j))],
    )(t3, right, y)
    for slot in range(slots):
        remote(slot, 0).wait_send()


def order_kernel(w, o):
    for p in range(2):
        for q in range(2):
            for j in range(8):
                o[j // 4, p * 2 + q, :, (j % 4) * 128 : (j % 4 + 1) * 128] = w[
                    pl.ds(p * 16 + j * 2 + q, o.shape[2], stride=32), :
                ]


def solution(mesh):
    def local_apply(wave_blk, left_rows, mpo_ten, right_rows):
        left = jnp.transpose(left_rows, (1, 0, 2))
        right = jnp.transpose(right_rows, (1, 0, 2))
        wave = jnp.transpose(wave_blk.reshape(512, 2, 2, 8, 128), (0, 1, 3, 2, 4)).reshape(512 * 32, 128)
        xs = pl.pallas_call(
            order_kernel,
            grid=(8,),
            in_specs=[pl.BlockSpec((64 * 32, 128), lambda i: (i, 0))],
            out_specs=pl.BlockSpec((2, 4, 64, 512), lambda i: (0, 0, i, 0)),
            out_shape=jax.ShapeDtypeStruct((2, 4, 512, 512), F32),
            name="order",
        )(wave)
        w2 = jnp.einsum("uspv,vtqr->rstupq", mpo_ten, mpo_ten, precision=HI, preferred_element_type=F32)
        mix = (w2.reshape(20, 1, 20, 1) * jnp.eye(8, dtype=F32).reshape(1, 8, 1, 8)).reshape(160, 160)

        t3, _, _, rfar = pl.pallas_call(
            left_kernel,
            in_specs=[ANY] * 4,
            out_specs=[ANY] * 4,
            out_shape=[
                jax.ShapeDtypeStruct((5, 4, 512, 1024), F32),
                jax.ShapeDtypeStruct((5, 4, 512, 1024), F32),
                jax.ShapeDtypeStruct((3, 2, 4, 512, 512), F32),
                jax.ShapeDtypeStruct((5, 1024, 1024), F32),
            ],
            scratch_shapes=[
                pltpu.VMEM((5, 4, 128, 256), F32),
                pltpu.VMEM((160, 160), F32),
                pltpu.SemaphoreType.DMA,
                pltpu.SemaphoreType.DMA((8,)),
                pltpu.SemaphoreType.DMA((8,)),
            ],
            compiler_params=pltpu.CompilerParams(
                collective_id=0, has_side_effects=True, vmem_limit_bytes=VMEM_LIMIT
            ),
            name="left_part",
        )(mix, left, xs, right)

        y = pl.pallas_call(
            right_kernel,
            in_specs=[ANY] * 3,
            out_specs=ANY,
            out_shape=jax.ShapeDtypeStruct((4, 512, 1024), F32),
            scratch_shapes=[
                pltpu.VMEM((4, 4, 128, 512), F32),
                pltpu.VMEM((8, 4, 128, 512), F32),
                pltpu.SemaphoreType.DMA((4,)),
                pltpu.SemaphoreType.DMA((8,)),
            ],
            compiler_params=pltpu.CompilerParams(
                collective_id=1, has_side_effects=True, vmem_limit_bytes=VMEM_LIMIT
            ),
            name="right_part",
        )(t3, rfar, right)
        return jnp.transpose(y, (1, 0, 2)).reshape(512, 2, 2, 1024)

    return jax.shard_map(
        local_apply,
        mesh=mesh,
        in_specs=(P("bx", None, None, "by"), P("bx", None, None), P(), P("by", None, None)),
        out_specs=P("bx", None, None, "by"),
        check_vma=False,
    )
```

time: 2280 us -> 668 us (0.29)
  matrix products: 1010 us -> 1.19 us
  blocking collectives: 784 us -> 0 us
  Pallas kernels: 0 us -> 642 us
  local copies, waits for them, and re-layouts: 272 us -> 17 us
  waiting for transfers between devices: 187 us -> 0 us
    dot_general x4 -> x1, matrix products: 1010 us -> 1.19 us  [local_apply(): jnp.einsum('uspv,vtqr->rstupq', mpo_ten, mpo_ten, precision=HI, preferred...]
    all_to_all x1 -> x0, blocking collectives: 784 us -> none  [local_apply(): right_cols = lax.all_to_all(right_rows, 'by', 2, 0, tiled=True)]
    pallas_call x0 -> x3, Pallas kernels: none -> 642 us  [the longest x1 333 us: local_apply(): pl.pallas_call(left_kernel, in_specs=[ANY] * 4, out_specs=[ANY] * 4, out_...]
    reduce_scatter x1 -> x0, waiting for transfers between devices: 187 us -> none  [local_apply(): return lax.psum_scatter(part_sum, 'by', scatter_dimension=3, tiled=True)]
    unnamed x4 -> x0, local copies, waits for them, and re-layouts: 92.4 us -> none
    all_to_all x1 -> x0, local copies, waits for them, and re-layouts: 58.5 us -> none  [local_apply(): right_cols = lax.all_to_all(right_rows, 'by', 2, 0, tiled=True)]
    transpose x1, local copies, waits for them, and re-layouts: 57.5 us -> 0.36 us  [local_apply(): jnp.einsum('uspv,vtqr->rstupq', mpo_ten, mpo_ten, precision=HI, preferred...]
    reshape x1, local copies, waits for them, and re-layouts: 48.7 us -> 15.4 us  [local_apply(): return jnp.transpose(y, (1, 0, 2)).reshape(512, 2, 2, 1024)]
  transfers between devices with their start and end apart: 2 -> 0, of which waited for: 1 -> 0; matrix products, arithmetic and copies ran while one was open for 7% -> 0% of each run, Pallas kernels for 0% -> 0%
where the time goes in v1:
time: 668 us; the launch traced here: 661 us
  Pallas kernels  642 us (96%)
  local copies, waits for them, and re-layouts  17 us (3%)
    pallas_call x1, Pallas kernels, local_apply(): pl.pallas_call(left_kernel, in_specs=[ANY] * 4, out_specs=[ANY] * 4, out_...  333 us
    pallas_call x1, Pallas kernels, local_apply(): pl.pallas_call(right_kernel, in_specs=[ANY] * 3, out_specs=ANY, out_shape...  299 us
    reshape x1, local copies, waits for them, and re-layouts, local_apply(): return jnp.transpose(y, (1, 0, 2)).reshape(512, 2, 2, 1024)  15.4 us

profile of v1, /device:TPU:0, one launch (start us, length us, event | category | flops | bytes accessed | tf_op | source)
XLA Modules:
  0.0 661.1 jit_solution(14714258404234366963)
XLA Ops:
  0.0 1.2 convolution_bitcast_fusion
  1.2 0.4 copy.11
  1.6 0.1 mul.19
  1.7 0.2 broadcast_multiply_fusion
  1.9 1.2 mul.23.mix_hbm
  3.1 10.4 %order.1.xs = f32[2,4,512,512]{3,2,1,0:T(8,128)} custom-call(f32[16384,128]{1,0:T(8,128)} %bitcast.21), custom_call_target="tpu_custom_call" | custom-call | tf_op jit(solution)/shard_map/order/pallas_call | solution.py:215
  13.5 333.4 %left_part.1 = (f32[5,4,512,1024]{3,2,1,0:T(8,128)}, f32[5,4,512,1024]{3,2,1,0:T(8,128)}, f32[3,2,4,512,512]{4,3,2,1,0:T(8,128)}, f32[5,1024,1024]{2,1,0:T(8,128)}) custom-call(f32[160,160]{1,0:T(8,128)} %mul.23.mix_hbm, f32[5,512,2048]{2,1,0:T(8,128)} %bitcast.20, f32[2,4,512,512]{3,2,1,0:T(8,128)} %order.1.xs, f32[5,1024,2048]{2,1,0:T(8,128)} %bitcast.17), custom_call_target="tpu_custom_call" | custom-call | tf_op jit(solution)/shard_map/left_part/pallas_call | solution.py:226
  346.9 298.6 %right_part.1 = f32[4,512,1024]{2,1,0:T(8,128)} custom-call(f32[5,4,512,1024]{3,2,1,0:T(8,128)} %get-tuple-element.7.t3, f32[5,1024,1024]{2,1,0:T(8,128)} %get-tuple-element.8.rfar, f32[5,1024,2048]{2,1,0:T(8,128)} %bitcast.18), custom_call_target="tpu_custom_call" | custom-call | tf_op jit(solution)/shard_map/right_part/pallas_call | solution.py:249
  645.5 15.4 %copy.13 = f32[512,2,2,1024]{3,2,1,0:T(2,128)} copy(f32[512,2,2,1024]{3,0,2,1:T(8,128)} %bitcast.19) | data formatting | bytes 16777216 | tf_op jit(solution)/shard_map/reshape | solution.py:265
  (1 shorter events, 0.0 us)

commit v2 on v1

v2 whole, which is shorter than its diff:
```python
import jax
import jax.numpy as jnp
from jax import lax
from jax.experimental import pallas as pl
from jax.experimental.pallas import tpu as pltpu
from jax.sharding import PartitionSpec as P

HI = lax.Precision.HIGHEST
F32 = jnp.float32
VMEM_LIMIT = 63 * 2**20
MESH = pl.DeviceIdType.MESH
ANY = pl.BlockSpec(memory_space=pl.ANY)


def greet(others):
    barrier = pltpu.get_barrier_semaphore()
    for other in others:
        pl.semaphore_signal(barrier, inc=1, device_id=other, device_id_type=MESH)
    pl.semaphore_wait(barrier, len(others))


def apply_kernel(
    mix_hbm, left, xs, right, y, t3, t1, xg, rfar, got, buf, mix, rbuf, held, gbuf, sem, rsem, send, recv, tsend, trecv
):
    ta, tf, kb, tb = 128, 256, 512, 512
    by = lax.axis_index("by")
    bx = lax.axis_index("bx")
    core = lax.rem(bx, 2)
    pair_bx = bx + 1 - 2 * core
    far_bx = lax.rem(bx + 2, 4)
    farpair_bx = lax.rem(pair_bx + 2, 4)
    pair = (by, pair_bx)
    far = (by, far_bx)
    across = (1 - by, bx)
    greet((pair, far, across))

    def remote(k, src, dst, to):
        return pltpu.make_async_remote_copy(
            src_ref=src, dst_ref=dst, send_sem=send.at[k], recv_sem=recv.at[k], device_id=to, device_id_type=MESH
        )

    def to_pair(k):
        cols = pl.ds(pl.multiple_of(k % 2 * tf, tf), tf)
        return remote(6 + k, xs.at[k // 2, :, :, cols], xg.at[0, k // 2, :, :, cols], pair)

    def to_far(h):
        return remote(h, xs.at[h], xg.at[1, h], far)

    def on_pair(h):
        return remote(2 + h, xg.at[1, h], xg.at[2, h], pair)

    rows = pl.ds(pl.multiple_of(core * 512, 512), 512)
    f_far = pl.ds(pl.multiple_of((1 - by) * 1024, 1024), 1024)
    f_own = pl.ds(pl.multiple_of(by * 1024, 1024), 1024)
    r_across = remote(4, right.at[:, rows, f_far], rfar.at[:, rows, :], across)
    r_pair = remote(5, rfar.at[:, rows, :], rfar.at[:, rows, :], pair)

    to_pair(0).start()
    to_far(0).start()
    r_across.start()
    for k in range(1, 4):
        to_pair(k).start()
    to_far(1).start()
    get_mix = pltpu.make_async_copy(mix_hbm, mix, sem.at[0])
    get_mix.start()
    to_pair(0).wait_recv()

    def right_far(n):
        src = rfar.at[:, pl.ds(pl.multiple_of(n * tb, tb), tb), :]
        return pltpu.make_async_copy(src, rbuf.at[n % 2], rsem.at[n % 2])

    def right_own(n):
        src = right.at[:, pl.ds(pl.multiple_of((n - 2) * tb, tb), tb), f_own]
        return pltpu.make_async_copy(src, rbuf.at[n % 2], rsem.at[n % 2])

    def product(l0, l1, x0, x1):
        lhs = jnp.concatenate([l0[...].reshape(5 * ta, kb), l1[...].reshape(5 * ta, kb)], axis=1)
        rhs = jnp.concatenate([jnp.concatenate([x[i] for i in range(4)], axis=1) for x in (x0, x1)], axis=0)
        return jnp.dot(lhs, rhs, precision=HI, preferred_element_type=F32)

    def left_spec(col):
        return pl.BlockSpec((5, ta, kb), lambda j, i: (0, i, col))

    x_spec = pl.BlockSpec((4, kb, tf), lambda j, i: (0, 0, j))

    def first_half(h, _):
        def body(l0, l1, x0, x1, o):
            step = pl.program_id(0) * 4 + pl.program_id(1)

            for k in range(1, 4):

                @pl.when(step + 8 * h == (1, 3, 6)[k - 1])
                def _(k=k):
                    to_pair(k).wait_recv()

            @pl.when(step + 8 * h == 13)
            def _():
                to_far(0).wait_recv()
                on_pair(0).start()

            d = product(l0, l1, x0, x1)
            for u in range(5):
                for i in range(4):
                    o[u, i] = d[u * ta : (u + 1) * ta, i * tf : (i + 1) * tf]

        t_spec = pl.BlockSpec((5, 4, ta, tf), lambda j, i: (0, 0, i, 2 * h + j))
        pltpu.emit_pipeline(
            body, grid=(2, 4), in_specs=[left_spec(bx), left_spec(pair_bx), x_spec, x_spec], out_specs=[t_spec]
        )(left, left, xs.at[h], xg.at[0, h], t1)
        return 0

    lax.fori_loop(0, 2, first_half, 0)

    def second_half(h, _):
        on_pair(h).wait_recv()

        def body(l0, l1, x0, x1, t, o):
            step = pl.program_id(0) * 4 + pl.program_id(1) + 8 * h

            @pl.when(step == 5)
            def _():
                to_far(1).wait_recv()
                on_pair(1).start()

            @pl.when(step == 11)
            def _():
                r_across.wait_recv()
                r_pair.start()

            @pl.when(step == 15)
            def _():
                r_pair.wait_recv()
                right_far(0).start()

            d = product(l0, l1, x0, x1)
            for u in range(5):
                for i in range(4):
                    buf[u, i] = d[u * ta : (u + 1) * ta, i * tf : (i + 1) * tf] + t[u, i]
            for a0 in range(0, ta, 16):
                m = jnp.concatenate(
                    [
                        jnp.concatenate([buf[u, i, a0 : a0 + 8], buf[u, i, a0 + 8 : a0 + 16]], axis=1)
                        for u in range(5)
                        for i in range(4)
                    ],
                    axis=0,
                )
                z = jnp.dot(mix[...], m, precision=HI, preferred_element_type=F32)
                for r in range(5):
                    for i in range(4):
                        row = (r * 4 + i) * 8
                        o[r, i, a0 : a0 + 8] = z[row : row + 8, :tf]
                        o[r, i, a0 + 8 : a0 + 16] = z[row : row + 8, tf:]

        t_spec = pl.BlockSpec((5, 4, ta, tf), lambda j, i: (0, 0, i, 2 * h + j))
        pltpu.emit_pipeline(
            body,
            grid=(2, 4),
            in_specs=[left_spec(far_bx), left_spec(farpair_bx), x_spec, x_spec, t_spec],
            out_specs=[t_spec],
        )(left, left, xg.at[1, h], xg.at[2, h], t1, t3)
        return 0

    get_mix.wait()
    lax.fori_loop(0, 2, second_half, 0)

    def tile_copy(tile):
        slot = lax.rem(tile, 4)
        return pltpu.make_async_remote_copy(
            src_ref=held.at[slot],
            dst_ref=got.at[tile],
            send_sem=tsend.at[slot],
            recv_sem=trecv.at[tile],
            device_id=across,
            device_id_type=MESH,
        )

    def right_body(t, o):
        n = pl.program_id(0)
        i = pl.program_id(1)
        tile = n * 4 + i
        slot = lax.rem(tile, 4)

        def block(k, act):
            @pl.when(jnp.logical_and(i == 0, n == k))
            def _():
                act()

        for k in range(4):

            def act(k=k):
                (right_far(k) if k < 2 else right_own(k)).wait()
                if k < 3:
                    (right_far(k + 1) if k + 1 < 2 else right_own(k + 1)).start()

            block(k, act)

        arrived = pltpu.make_async_copy(got.at[jnp.maximum(tile - 8, 0)], gbuf, sem.at[1])

        @pl.when(jnp.logical_and(tile >= 4, n < 2))
        def _():
            tile_copy(tile - 4).wait_send()

        @pl.when(n >= 2)
        def _():
            tile_copy(tile - 8).wait_recv()
            arrived.start()

        lhs = jnp.concatenate([t[r].reshape(4 * ta, 1024) for r in range(5)], axis=1)
        half = lax.rem(n, 2)
        rhs = jnp.concatenate([rbuf[half, r] for r in range(5)], axis=1)
        d = lax.dot_general(lhs, rhs, (((1,), (1,)), ((), ())), precision=HI, preferred_element_type=F32)
        o[...] = d.reshape(4, ta, tb)

        @pl.when(n < 2)
        def _():
            held[slot] = o[...]
            tile_copy(tile).start()

        @pl.when(n >= 2)
        def _():
            arrived.wait()
            o[...] += gbuf[...]

    pltpu.emit_pipeline(
        right_body,
        grid=(4, 4),
        in_specs=[pl.BlockSpec((5, 4, ta, 1024), lambda n, i: (0, 0, i, 0))],
        out_specs=[pl.BlockSpec((4, ta, tb), lambda n, i: (0, (n // 2) * i, (n // 2) * (n - 2)))],
    )(t3, y)
    for tile in range(4, 8):
        tile_copy(tile).wait_send()
    for k in range(4):
        to_pair(k).wait_send()
    for h in range(2):
        to_far(h).wait_send()
        on_pair(h).wait_send()
    r_across.wait_send()
    r_pair.wait_send()


PITCH = 40


def order_kernel(w, o, raw, sem):
    step = pl.program_id(0)
    cs = raw.shape[1]

    def fetch(k):
        return pltpu.make_async_copy(
            w.at[pl.ds(k * cs, cs)], raw.at[lax.rem(k, 2), :, 0:32, :], sem.at[lax.rem(k, 2)]
        )

    @pl.when(step == 0)
    def _():
        fetch(0).start()

    @pl.when(step + 1 < pl.num_programs(0))
    def _():
        fetch(step + 1).start()

    fetch(step).wait()
    flat = raw.at[lax.rem(step, 2)].reshape(cs * PITCH, 128)
    for p in range(2):
        for q in range(2):
            for j in range(8):
                o[j // 4, p * 2 + q, :, (j % 4) * 128 : (j % 4 + 1) * 128] = flat[
                    pl.ds(p * 16 + j * 2 + q, cs, stride=PITCH), :
                ]


def place_kernel(y, o, raw, sem):
    step = pl.program_id(0)
    cs = raw.shape[1]

    def store(k):
        return pltpu.make_async_copy(
            raw.at[lax.rem(k, 2), :, 0:32, :], o.at[pl.ds(k * cs, cs)], sem.at[lax.rem(k, 2)]
        )

    @pl.when(step >= 2)
    def _():
        store(step - 2).wait()

    flat = raw.at[lax.rem(step, 2)].reshape(cs * PITCH, 128)
    for s in range(2):
        for t in range(2):
            for j in range(8):
                flat[pl.ds(s * 16 + j * 2 + t, cs, stride=PITCH), :] = y[s * 2 + t, :, j * 128 : (j + 1) * 128]
    store(step).start()

    @pl.when(step + 1 == pl.num_programs(0))
    def _():
        store(step - 1).wait()
        store(step).wait()


def solution(mesh):
    def local_apply(wave_blk, left_rows, mpo_ten, right_rows):
        left = jnp.transpose(left_rows, (1, 0, 2))
        right = jnp.transpose(right_rows, (1, 0, 2))
        wave = jnp.transpose(wave_blk.reshape(512, 2, 2, 8, 128), (0, 1, 3, 2, 4)).reshape(512, 32, 128)
        cs = 128
        edge = [pltpu.VMEM((2, cs, PITCH, 128), F32), pltpu.SemaphoreType.DMA((2,))]
        xs = pl.pallas_call(
            order_kernel,
            grid=(512 // cs,),
            in_specs=[ANY],
            out_specs=pl.BlockSpec((2, 4, cs, 512), lambda i: (0, 0, i, 0)),
            out_shape=jax.ShapeDtypeStruct((2, 4, 512, 512), F32),
            scratch_shapes=edge,
            name="order",
        )(wave)
        w2 = jnp.einsum("uspv,vtqr->rstupq", mpo_ten, mpo_ten, precision=HI, preferred_element_type=F32)
        mix = (w2.reshape(20, 1, 20, 1) * jnp.eye(8, dtype=F32).reshape(1, 8, 1, 8)).reshape(160, 160)

        y = pl.pallas_call(
            apply_kernel,
            in_specs=[ANY] * 4,
            out_specs=[ANY] * 6,
            out_shape=[
                jax.ShapeDtypeStruct((4, 512, 1024), F32),
                jax.ShapeDtypeStruct((5, 4, 512, 1024), F32),
                jax.ShapeDtypeStruct((5, 4, 512, 1024), F32),
                jax.ShapeDtypeStruct((3, 2, 4, 512, 512), F32),
                jax.ShapeDtypeStruct((5, 1024, 1024), F32),
                jax.ShapeDtypeStruct((8, 4, 128, 512), F32),
            ],
            scratch_shapes=[
                pltpu.VMEM((5, 4, 128, 256), F32),
                pltpu.VMEM((160, 160), F32),
                pltpu.VMEM((2, 5, 512, 1024), F32),
                pltpu.VMEM((4, 4, 128, 512), F32),
                pltpu.VMEM((4, 128, 512), F32),
                pltpu.SemaphoreType.DMA((2,)),
                pltpu.SemaphoreType.DMA((2,)),
                pltpu.SemaphoreType.DMA((10,)),
                pltpu.SemaphoreType.DMA((10,)),
                pltpu.SemaphoreType.DMA((4,)),
                pltpu.SemaphoreType.DMA((8,)),
            ],
            compiler_params=pltpu.CompilerParams(
                collective_id=0, has_side_effects=True, vmem_limit_bytes=VMEM_LIMIT
            ),
            name="apply",
        )(mix, left, xs, right)[0]

        out = pl.pallas_call(
            place_kernel,
            grid=(512 // cs,),
            in_specs=[pl.BlockSpec((4, cs, 1024), lambda i: (0, i, 0))],
            out_specs=ANY,
            out_shape=jax.ShapeDtypeStruct((512, 32, 128), F32),
            scratch_shapes=edge,
            name="place",
        )(y)
        return jnp.transpose(out.reshape(512, 2, 8, 2, 128), (0, 1, 3, 2, 4)).reshape(512, 2, 2, 1024)

    return jax.shard_map(
        local_apply,
        mesh=mesh,
        in_specs=(P("bx", None, None, "by"), P("bx", None, None), P(), P("by", None, None)),
        out_specs=P("bx", None, None, "by"),
        check_vma=False,
    )
```

time: 668 us -> 631 us (0.945)
  Pallas kernels: 642 us -> 616 us
  local copies, waits for them, and re-layouts: 17 us -> 1.65 us
    pallas_call x3, Pallas kernels: 642 us -> 616 us  [the longest x1 601 us: local_apply(): pl.pallas_call(apply_kernel, in_specs=[ANY] * 4, out_specs=[ANY] * 6, out...]
    reshape x1 -> x0, local copies, waits for them, and re-layouts: 15.4 us -> none  [local_apply(): return jnp.transpose(y, (1, 0, 2)).reshape(512, 2, 2, 1024)]
where the time goes in v2:
time: 631 us; the launch traced here: 620 us
  Pallas kernels  616 us (98%)
    pallas_call x1, Pallas kernels, local_apply(): pl.pallas_call(apply_kernel, in_specs=[ANY] * 4, out_specs=[ANY] * 6, out...  601 us

profile of v2, /device:TPU:0, one launch (start us, length us, event | category | flops | bytes accessed | tf_op | source)
XLA Modules:
  0.0 619.9 jit_solution(4361427815748012554)
XLA Ops:
  0.0 1.2 convolution_bitcast_fusion
  1.2 0.4 copy.11
  1.6 0.1 mul.19
  1.7 0.2 broadcast_multiply_fusion
  1.9 1.2 mul.23.mix_hbm
  3.1 7.5 %order.1.xs = f32[2,4,512,512]{3,2,1,0:T(8,128)} custom-call(f32[512,32,128]{2,1,0:T(8,128)} %bitcast.21), custom_call_target="tpu_custom_call" | custom-call | tf_op jit(solution)/shard_map/order/pallas_call | solution.py:305
  10.6 601.1 %apply.1 = (f32[4,512,1024]{2,1,0:T(8,128)}, f32[5,4,512,1024]{3,2,1,0:T(8,128)}, f32[5,4,512,1024]{3,2,1,0:T(8,128)}, f32[3,2,4,512,512]{4,3,2,1,0:T(8,128)}, f...) custom-call(f32[160,160]{1,0:T(8,128)} %mul.23.mix_hbm, f32[5,512,2048]{2,1,0:T(8,128)} %bitcast.20, ...), custom_call_target="tpu_custom_call" | custom-call | tf_op jit(solution)/shard_map/apply/pallas_call | solution.py:317
  611.7 7.8 %place.1 = f32[512,32,128]{2,1,0:T(8,128)} custom-call(f32[4,512,1024]{2,1,0:T(8,128)} %get-tuple-element.6.y), custom_call_target="tpu_custom_call" | custom-call | tf_op jit(solution)/shard_map/place/pallas_call | solution.py:348
  (1 shorter events, 0.0 us)

commit v3 on v2

--- a/solution.py
+++ b/solution.py
@@ -20,7 +20,7 @@
 
 
 def apply_kernel(
-    mix_hbm, left, xs, right, y, t3, t1, xg, rfar, got, buf, mix, rbuf, held, gbuf, sem, rsem, send, recv, tsend, trecv
+    mix_hbm, left, xs, right, y, t3, xg, rfar, got, tbuf, mix, rbuf, held, gbuf, sem, rsem, send, recv, tsend, trecv
 ):
     ta, tf, kb, tb = 128, 256, 512, 512
     by = lax.axis_index("by")
@@ -41,13 +41,13 @@
 
     def to_pair(k):
         cols = pl.ds(pl.multiple_of(k % 2 * tf, tf), tf)
-        return remote(6 + k, xs.at[k // 2, :, :, cols], xg.at[0, k // 2, :, :, cols], pair)
+        return remote(6 + k, xg.at[0, k // 2, :, :, cols], xg.at[1, k // 2, :, :, cols], pair)
 
     def to_far(h):
-        return remote(h, xs.at[h], xg.at[1, h], far)
+        return remote(h, xg.at[0, h], xg.at[2, h], far)
 
     def on_pair(h):
-        return remote(2 + h, xg.at[1, h], xg.at[2, h], pair)
+        return remote(2 + h, xg.at[2, h], xg.at[3, h], pair)
 
     rows = pl.ds(pl.multiple_of(core * 512, 512), 512)
     f_far = pl.ds(pl.multiple_of((1 - by) * 1024, 1024), 1024)
@@ -73,96 +73,103 @@
         src = right.at[:, pl.ds(pl.multiple_of((n - 2) * tb, tb), tb), f_own]
         return pltpu.make_async_copy(src, rbuf.at[n % 2], rsem.at[n % 2])
 
-    def product(l0, l1, x0, x1):
-        lhs = jnp.concatenate([l0[...].reshape(5 * ta, kb), l1[...].reshape(5 * ta, kb)], axis=1)
-        rhs = jnp.concatenate([jnp.concatenate([x[i] for i in range(4)], axis=1) for x in (x0, x1)], axis=0)
-        return jnp.dot(lhs, rhs, precision=HI, preferred_element_type=F32)
-
-    def left_spec(col):
-        return pl.BlockSpec((5, ta, kb), lambda j, i: (0, i, col))
-
     x_spec = pl.BlockSpec((4, kb, tf), lambda j, i: (0, 0, j))
 
-    def first_half(h, _):
+    def left_half(part, _):
+        s = part // 2
+        h = lax.rem(part, 2)
+        col0 = (1 - s) * bx + s * far_bx
+        col1 = (1 - s) * pair_bx + s * farpair_bx
+
+        @pl.when(part == 2)
+        def _():
+            get_mix.wait()
+            on_pair(0).wait_recv()
+
+        @pl.when(part == 3)
+        def _():
+            on_pair(1).wait_recv()
+
         def body(l0, l1, x0, x1, o):
-            step = pl.program_id(0) * 4 + pl.program_id(1)
-
-            for k in range(1, 4):
-
-                @pl.when(step + 8 * h == (1, 3, 6)[k - 1])
-                def _(k=k):
-                    to_pair(k).wait_recv()
-
-            @pl.when(step + 8 * h == 13)
-            def _():
-                to_far(0).wait_recv()
-                on_pair(0).start()
-
-            d = product(l0, l1, x0, x1)
-            for u in range(5):
-                for i in range(4):
-                    o[u, i] = d[u * ta : (u + 1) * ta, i * tf : (i + 1) * tf]
-
-        t_spec = pl.BlockSpec((5, 4, ta, tf), lambda j, i: (0, 0, i, 2 * h + j))
-        pltpu.emit_pipeline(
-            body, grid=(2, 4), in_specs=[left_spec(bx), left_spec(pair_bx), x_spec, x_spec], out_specs=[t_spec]
-        )(left, left, xs.at[h], xg.at[0, h], t1)
-        return 0
-
-    lax.fori_loop(0, 2, first_half, 0)
-
-    def second_half(h, _):
-        on_pair(h).wait_recv()
-
-        def body(l0, l1, x0, x1, t, o):
-            step = pl.program_id(0) * 4 + pl.program_id(1) + 8 * h
-
-            @pl.when(step == 5)
-            def _():
-                to_far(1).wait_recv()
-                on_pair(1).start()
-
-            @pl.when(step == 11)
-            def _():
+            j = pl.program_id(0)
+            i = pl.program_id(1)
+            step = part * 8 + j * 4 + i
+
+            def at(n, act):
+                @pl.when(step == n)
+                def _():
+                    act()
+
+            def on_far(k):
+                to_far(k).wait_recv()
+                on_pair(k).start()
+
+            def on_right():
                 r_across.wait_recv()
                 r_pair.start()
 
-            @pl.when(step == 15)
-            def _():
+            def first_right():
                 r_pair.wait_recv()
                 right_far(0).start()
 
-            d = product(l0, l1, x0, x1)
+            at(1, to_pair(1).wait_recv)
+            at(3, to_pair(2).wait_recv)
+            at(6, to_pair(3).wait_recv)
+            at(13, lambda: on_far(0))
+            at(21, lambda: on_far(1))
+            at(27, on_right)
+            at(31, first_right)
+
+            rows_i = pl.ds(pl.multiple_of(i * ta, ta), ta)
+            cols_j = pl.ds(pl.multiple_of((2 * h + j) * tf, tf), tf)
+            get_t = pltpu.make_async_copy(t3.at[:, :, rows_i, cols_j], tbuf, sem.at[1])
+
+            @pl.when(s == 1)
+            def _():
+                get_t.start()
+
+            lhs = jnp.concatenate([l0[...].reshape(5 * ta, kb), l1[...].reshape(5 * ta, kb)], axis=1)
+            rhs = jnp.concatenate([jnp.concatenate([x[n] for n in range(4)], axis=1) for x in (x0, x1)], axis=0)
+            d = jnp.dot(lhs, rhs, precision=HI, preferred_element_type=F32)
             for u in range(5):
-                for i in range(4):
-                    buf[u, i] = d[u * ta : (u + 1) * ta, i * tf : (i + 1) * tf] + t[u, i]
-            for a0 in range(0, ta, 16):
-                m = jnp.concatenate(
-                    [
-                        jnp.concatenate([buf[u, i, a0 : a0 + 8], buf[u, i, a0 + 8 : a0 + 16]], axis=1)
-                        for u in range(5)
-                        for i in range(4)
-                    ],
-                    axis=0,
-                )
-                z = jnp.dot(mix[...], m, precision=HI, preferred_element_type=F32)
-                for r in range(5):
-                    for i in range(4):
-                        row = (r * 4 + i) * 8
-                        o[r, i, a0 : a0 + 8] = z[row : row + 8, :tf]
-                        o[r, i, a0 + 8 : a0 + 16] = z[row : row + 8, tf:]
-
-        t_spec = pl.BlockSpec((5, 4, ta, tf), lambda j, i: (0, 0, i, 2 * h + j))
+                for n in range(4):
+                    o[u, n] = d[u * ta : (u + 1) * ta, n * tf : (n + 1) * tf]
+
+            @pl.when(s == 1)
+            def _():
+                get_t.wait()
+                for a0 in range(0, ta, 16):
+                    m = jnp.concatenate(
+                        [
+                            jnp.concatenate(
+                                [o[u, n, b : b + 8] + tbuf[u, n, b : b + 8] for b in (a0, a0 + 8)], axis=1
+                            )
+                            for u in range(5)
+                            for n in range(4)
+                        ],
+                        axis=0,
+                    )
+                    z = jnp.dot(mix[...], m, precision=HI, preferred_element_type=F32)
+                    for r in range(5):
+                        for n in range(4):
+                            row = (r * 4 + n) * 8
+                            o[r, n, a0 : a0 + 8] = z[row : row + 8, :tf]
+                            o[r, n, a0 + 8 : a0 + 16] = z[row : row + 8, tf:]
+
         pltpu.emit_pipeline(
             body,
             grid=(2, 4),
-            in_specs=[left_spec(far_bx), left_spec(farpair_bx), x_spec, x_spec, t_spec],
-            out_specs=[t_spec],
-        )(left, left, xg.at[1, h], xg.at[2, h], t1, t3)
+            in_specs=[
+                pl.BlockSpec((5, ta, kb), lambda j, i: (0, i, col0)),
+                pl.BlockSpec((5, ta, kb), lambda j, i: (0, i, col1)),
+                x_spec,
+                x_spec,
+            ],
+            out_specs=[pl.BlockSpec((5, 4, ta, tf), lambda j, i: (0, 0, i, 2 * h + j))],
+        )(left, left, xg.at[2 * s, h], xg.at[2 * s + 1, h], t3)
         return 0
 
-    get_mix.wait()
-    lax.fori_loop(0, 2, second_half, 0)
+    lax.fori_loop(0, 4, left_half, 0)
 
     def tile_copy(tile):
         slot = lax.rem(tile, 4)
@@ -264,7 +271,7 @@
     for p in range(2):
         for q in range(2):
             for j in range(8):
-                o[j // 4, p * 2 + q, :, (j % 4) * 128 : (j % 4 + 1) * 128] = flat[
+                o[0, j // 4, p * 2 + q, :, (j % 4) * 128 : (j % 4 + 1) * 128] = flat[
                     pl.ds(p * 16 + j * 2 + q, cs, stride=PITCH), :
                 ]
 
@@ -306,8 +313,8 @@
             order_kernel,
             grid=(512 // cs,),
             in_specs=[ANY],
-            out_specs=pl.BlockSpec((2, 4, cs, 512), lambda i: (0, 0, i, 0)),
-            out_shape=jax.ShapeDtypeStruct((2, 4, 512, 512), F32),
+            out_specs=pl.BlockSpec((1, 2, 4, cs, 512), lambda i: (0, 0, 0, i, 0)),
+            out_shape=jax.ShapeDtypeStruct((4, 2, 4, 512, 512), F32),
             scratch_shapes=edge,
             name="order",
         )(wave)
@@ -317,15 +324,15 @@
         y = pl.pallas_call(
             apply_kernel,
             in_specs=[ANY] * 4,
-            out_specs=[ANY] * 6,
+            out_specs=[ANY] * 5,
             out_shape=[
                 jax.ShapeDtypeStruct((4, 512, 1024), F32),
                 jax.ShapeDtypeStruct((5, 4, 512, 1024), F32),
-                jax.ShapeDtypeStruct((5, 4, 512, 1024), F32),
-                jax.ShapeDtypeStruct((3, 2, 4, 512, 512), F32),
+                jax.ShapeDtypeStruct((4, 2, 4, 512, 512), F32),
                 jax.ShapeDtypeStruct((5, 1024, 1024), F32),
                 jax.ShapeDtypeStruct((8, 4, 128, 512), F32),
             ],
+            input_output_aliases={2: 2},
             scratch_shapes=[
                 pltpu.VMEM((5, 4, 128, 256), F32),
                 pltpu.VMEM((160, 160), F32),

time: 631 us -> 620 us (0.983); the launches traced: 620 us -> 620 us
  no operation moved by 1% of the time
where the time goes in v3:
time: 620 us
  Pallas kernels  617 us (100%)
    pallas_call x1, Pallas kernels, local_apply(): pl.pallas_call(apply_kernel, in_specs=[ANY] * 4, out_specs=[ANY] * 5, out...  601 us

profile of v3, /device:TPU:0, one launch (start us, length us, event | category | flops | bytes accessed | tf_op | source)
XLA Modules:
  0.0 619.8 jit_solution(17565692309014568327)
XLA Ops:
  0.0 1.2 convolution_bitcast_fusion
  1.2 0.4 copy.12
  1.6 0.1 mul.19
  1.7 0.2 broadcast_multiply_fusion
  1.9 1.2 mul.23.mix_hbm
  3.1 7.5 %order.1.xs = f32[4,2,4,512,512]{4,3,2,1,0:T(8,128)} custom-call(f32[512,32,128]{2,1,0:T(8,128)} %bitcast.21), custom_call_target="tpu_custom_call" | custom-call | tf_op jit(solution)/shard_map/order/pallas_call | solution.py:312
  10.5 601.3 %apply.1 = (f32[4,512,1024]{2,1,0:T(8,128)}, f32[5,4,512,1024]{3,2,1,0:T(8,128)}, f32[4,2,4,512,512]{4,3,2,1,0:T(8,128)}, f32[5,1024,1024]{2,1,0:T(8,128)}, f32[8,4,128,512]{3,2,1,0:T(8,128)}) custom-call(f32[160,160]{1,0:T(8,128)} %mul.23.mix_hbm, f32[5,512,2048]{2,1,0:T(8,128)} %bitcast.20, ...), custom_call_target="tpu_custom_call", output_to_operand_aliasing={{2}: (2, {})} | custom-call | tf_op jit(solution)/shard_map/apply/pallas_call | solution.py:324
  611.9 7.8 %place.1 = f32[512,32,128]{2,1,0:T(8,128)} custom-call(f32[4,512,1024]{2,1,0:T(8,128)} %get-tuple-element.6.y), custom_call_target="tpu_custom_call" | custom-call | tf_op jit(solution)/shard_map/place/pallas_call | solution.py:355
  (1 shorter events, 0.0 us)
